TPU v7x, 256 devices: a whole 4x4x8 slice. The times are simulated.
256 devices in a mesh: dp: 64 (over x, z, y_hi), mp: 4 (over y_lo, core).
Axes of the slice: x: 4, y: 4 (y_hi: 2, y_lo: 2; y = y_hi * 2 + y_lo), z: 8, core: 2. Of those that a mesh axis runs over, the one named last changes fastest.
Arguments:
- media: bfloat16 [128, 8, 256, 1024], P('dp'), may hold values from -6 to 6
- latents: bfloat16 [64, 1024], replicated, may hold values from -6 to 6
- time_embed: bfloat16 [8, 1024], replicated, may hold values from -5 to 5
- media_gain: float32 [2, 1024], replicated, may hold values from 0.25 to 1.75
- latent_gain: float32 [2, 1024], replicated, may hold values from 0.25 to 1.75
- ffn_gain: float32 [2, 1024], replicated, may hold values from 0.25 to 1.75
- out_gain: float32 [1024], replicated, may hold values from 0.25 to 1.75
- w_query: bfloat16 [2, 1024, 512], P(None, 'dp', 'mp'), may hold values from -0.1875 to 0.1875
- w_key: bfloat16 [2, 1024, 512], P(None, 'dp', 'mp'), may hold values from -0.1875 to 0.1875
- w_value: bfloat16 [2, 1024, 512], P(None, 'dp', 'mp'), may hold values from -0.1875 to 0.1875
- w_out: bfloat16 [2, 512, 1024], P(None, 'mp', 'dp'), may hold values from -0.25 to 0.25
- w_up: bfloat16 [2, 1024, 4096], P(None, 'dp', 'mp'), may hold values from -0.1875 to 0.1875
- w_down: bfloat16 [2, 4096, 1024], P(None, 'mp', 'dp'), may hold values from -0.09375 to 0.09375
Outputs:
- resampled: bfloat16 [128, 64, 1024], P('dp')
All inputs are finite; a program needn't handle non-finite values.
Results may differ from a plain program's by a relative error of at most 0.013.
Values may be sent and summed in bfloat16 or wider, within the bound.
No kernel may reach another device: no remote copies, remote signals or barrier semaphores. Data moves between devices by JAX's collectives and lax.ppermute only.
A program may use at most 128 MiB of HBM per device.

v0:
```python
import jax
import jax.numpy as jnp
from jax import lax
from jax.sharding import PartitionSpec as P

HEAD = 64
LAYERS = 2


def in_one_piece(arrays, axis, dim, along):
    widths = [a.shape[along] for a in arrays]
    both = jnp.concatenate(arrays, axis=along)
    filled = lax.all_gather(both, axis, axis=dim, tiled=True)
    return tuple(jnp.split(filled, [sum(widths[:k]) for k in range(1, len(widths))], axis=along))


def copy_for_each(x, axis):
    copies = jnp.broadcast_to(x, (lax.axis_size(axis), *x.shape))
    return lax.all_to_all(copies, axis, split_axis=0, concat_axis=0, tiled=True)


def of_everyone(x, axis):
    everything = copy_for_each(x, axis)
    return jnp.sum(everything.astype(jnp.float32), axis=0)


def layer_norm(values, gain):
    center = values - jnp.mean(values, axis=-1, keepdims=True)
    spread = jnp.mean(center * center, axis=-1, keepdims=True)
    return center * lax.rsqrt(spread + 1e-05) * gain


def matmul(left, right):
    return jnp.dot(left, right, preferred_element_type=jnp.float32)


def on_device(
    media,
    latents,
    time_embed,
    media_gain,
    latent_gain,
    ffn_gain,
    out_gain,
    w_query,
    w_key,
    w_value,
    w_out,
    w_up,
    w_down,
):
    samples = media.shape[0]
    frames = media.shape[1]
    patches = media.shape[2]
    width = media.shape[3]
    count = latents.shape[0]
    head_size = HEAD
    local_heads = w_query.shape[2] // head_size
    scale = head_size ** (-0.5)
    tokens = frames * patches
    flat = (media.astype(jnp.float32) + time_embed.astype(jnp.float32)[None, :, None, :]).reshape(
        samples * tokens, width
    )
    state = jnp.broadcast_to(latents.astype(jnp.float32)[None], (samples, count, width)).reshape(
        samples * count, width
    )
    row_parts = in_one_piece((w_query, w_key, w_value, w_up), "dp", 1, 2)
    col_parts = (
        lax.all_gather(w_out, "dp", axis=2, tiled=True),
        lax.all_gather(w_down, "dp", axis=2, tiled=True),
    )

    def full_rows(values, gain):
        normed = layer_norm(values, gain).astype(jnp.bfloat16)
        return normed

    def add_update(current, partial_value):
        return current + of_everyone(partial_value.astype(jnp.bfloat16), "mp").astype(jnp.float32)

    for layer in range(LAYERS):
        query_weight = row_parts[0][layer]
        key_weight = row_parts[1][layer]
        value_weight = row_parts[2][layer]
        up_weight = row_parts[3][layer]
        out_weight = col_parts[0][layer]
        down_weight = col_parts[1][layer]
        media_normed = layer_norm(flat, media_gain[layer]).astype(jnp.bfloat16)
        latent_normed = full_rows(state, latent_gain[layer])
        query = matmul(latent_normed, query_weight)
        key_media = matmul(media_normed, key_weight)
        value_media = matmul(media_normed, value_weight)
        key_latent = matmul(latent_normed, key_weight)
        value_latent = matmul(latent_normed, value_weight)
        queries = (
            (query * scale).astype(jnp.bfloat16).reshape(samples, count, local_heads, head_size)
        )
        keys = jnp.concatenate(
            [
                key_media.astype(jnp.bfloat16).reshape(samples, tokens, local_heads, head_size),
                key_latent.astype(jnp.bfloat16).reshape(samples, count, local_heads, head_size),
            ],
            axis=1,
        )
        values = jnp.concatenate(
            [
                value_media.astype(jnp.bfloat16).reshape(samples, tokens, local_heads, head_size),
                value_latent.astype(jnp.bfloat16).reshape(samples, count, local_heads, head_size),
            ],
            axis=1,
        )
        scores = jnp.einsum("sqhd,skhd->shqk", queries, keys, preferred_element_type=jnp.float32)
        probs = jax.nn.softmax(scores, axis=-1).astype(jnp.bfloat16)
        attended = jnp.einsum("shqk,skhd->sqhd", probs, values, preferred_element_type=jnp.float32)
        attended = attended.astype(jnp.bfloat16).reshape(samples * count, local_heads * head_size)
        state = add_update(state, matmul(attended, out_weight))
        ffn_normed = full_rows(state, ffn_gain[layer])
        hidden = jax.nn.gelu(matmul(ffn_normed, up_weight), approximate=False).astype(jnp.bfloat16)
        state = add_update(state, matmul(hidden, down_weight))
    final = layer_norm(state, out_gain).astype(jnp.bfloat16)
    return final.reshape(samples, count, width)


def solution(mesh):
    in_specs = (
        P("dp", None, None, None),
        P(),
        P(),
        P(),
        P(),
        P(),
        P(),
        P(None, "dp", "mp"),
        P(None, "dp", "mp"),
        P(None, "dp", "mp"),
        P(None, "mp", "dp"),
        P(None, "dp", "mp"),
        P(None, "mp", "dp"),
    )
    out_specs = P("dp", None, None)
    return jax.shard_map(
        on_device, mesh=mesh, in_specs=in_specs, out_specs=out_specs, check_vma=False
    )
```

profile of v0, /device:TPU:32, one launch (start us, length us, event | category | flops | bytes accessed | tf_op | source)
XLA Modules:
  0.0 386.2 jit_solution(2744716518895289468)
XLA Ops:
  6.5 1.5 pad_maximum_fusion
  13.3 5.3 %fusion.3 = f32[2,8,256]{2,1,0:T(8,128)S(1)} fusion(bf16[2,8,256,1024]{3,2,1,0:T(8,128)(2,1)} %param.13, f32[8,1024]{1,0:T(8,128)S(1)} %convert_element_type.171), kind=kLoop, calls=%fused_computation.7 | loop fusion | flops 12578816 | bytes 8437760 | tf_op jit(solution)/shard_map/reduce_sum | solution.py:28
  19.1 3.2 multiply_reduce_fusion
  22.4 183.6 %all_gather.10 = bf16[2,128,1024]{1,2,0:T(8,128)(2,1)S(1)} all-gather(bf16[2,128,16]{1,2,0:T(8,128)(2,1)S(1)} %copy-done.1), channel_id=1, replica_groups=mesh['dp'=64,'mp'=4] {'dp'}, dimensions={2}, use_global_device_ids=true | all-gather | bytes 532480 | tf_op jit(solution)/shard_map/all_gather | solution.py:69
  206.1 7.3 %multiply_convert_fusion = (bf16[2,8,256,1024]{3,2,1,0:T(8,128)(2,1)}, bf16[2,8,256,1024]{3,2,1,0:T(8,128)(2,1)}) fusion(bf16[2,8,256,1024]{3,2,1,0:T(8,128)(2,1)S(1)} %copy-done, f32[1024]{0:T(1024)S(1)} %bitcast.118, f32[2,8,256]{2,1,0:T(8,128)S(1)} %add_rsqrt_fusion, f32[2,8,256]{2,1,0:T(8,128)S(1)} %broadcast_multiply_fusion, ...), kind=kLoop, calls=%fused_computation.2 | loop fusion | flops 33554432 | bytes 25239552 | tf_op jit(solution)/shard_map/convert_element_type | solution.py:87
  213.3 1.2 convolution_convert_fusion.10
  216.0 6.8 %convolution_convert_fusion.2 = bf16[4096,128]{1,0:T(8,128)(2,1)} fusion(bf16[4096,1024]{1,0:T(8,128)(2,1)} %bitcast.100, bf16[2,1024,1408]{2,1,0:T(8,128)(2,1)} %all-gather.3.cloned.1.call-done), kind=kOutput, calls=%fused_computation.11 | convolution fusion | flops 1074266112 | bytes 9699328 | tf_op jit(solution)/shard_map/dot_general | solution.py:34
  222.7 3.9 %reshape.1012 = bf16[2,2048,2,64]{3,2,1,0:T(2,128)(2,1)S(1)} reshape(bf16[4096,128]{1,0:T(8,128)(2,1)} %convolution_convert_fusion.2) | data formatting | bytes 2097152 | tf_op jit(solution)/shard_map/reshape | solution.py:99
  226.6 3.6 copy.44
  231.5 6.7 %convolution_convert_fusion.3 = bf16[4096,128]{1,0:T(8,128)(2,1)} fusion(bf16[4096,1024]{1,0:T(8,128)(2,1)} %bitcast.101, bf16[2,1024,1408]{2,1,0:T(8,128)(2,1)} %all-gather.3.cloned.1.call-done), kind=kOutput, calls=%fused_computation.12 | convolution fusion | flops 1074266112 | bytes 9699328 | tf_op jit(solution)/shard_map/dot_general | solution.py:34
  238.3 3.9 %reshape.1011 = bf16[2,2048,2,64]{3,2,1,0:T(2,128)(2,1)S(1)} reshape(bf16[4096,128]{1,0:T(8,128)(2,1)} %convolution_convert_fusion.3) | data formatting | bytes 2097152 | tf_op jit(solution)/shard_map/reshape | solution.py:106
  242.1 3.5 copy.41
  245.6 3.3 fusion.215
  248.9 2.5 fusion.15
  251.9 1.2 broadcast_in_dim.13
  253.1 3.7 all-to-all-start
  256.9 14.2 %all-to-all-done = bf16[4,128,1024]{2,1,0:T(8,128)(2,1)S(1)} async-done(((bf16[4,128,1024]{2,1,0:T(8,128)(2,1)}), bf16[4,128,1024]{2,1,0:T(8,128)(2,1)S(1)}, u32[]{:S(2)}, u32[]{:S(2)}) %all-to-all-start) | async-done | bytes 1048608 | tf_op jit(solution)/shard_map/all_to_all | solution.py:19
  271.9 15.6 %all-gather.5.cloned.1.call-done = bf16[2,1024,1024]{1,2,0:T(8,128)(2,1)} async-done(((bf16[2,1024,16]{1,2,0:T(8,128)(2,1)}), bf16[2,1024,1024]{1,2,0:T(8,128)(2,1)}) %all-gather.5.cloned.1.call-update) | async-done | bytes 4194320 | tf_op jit(solution)/shard_map/all_gather | solution.py:70
  287.5 4.4 %fusion.13 = bf16[128,1024]{1,0:T(8,128)(2,1)S(1)} fusion(bf16[2,1024,1024]{1,2,0:T(8,128)(2,1)} %all-gather.5.cloned.1.call-done, bf16[128,1024]{1,0:T(8,128)(2,1)S(1)} %bitcast.113, bf16[2,1024,1408]{2,1,0:T(8,128)(2,1)} %all-gather.3.cloned.1.call-done), kind=kOutput, calls=%fused_computation.31 | convolution fusion | flops 545521664 | bytes 4718592 | tf_op jit(solution)/shard_map/dot_general | solution.py:34
  293.0 4.2 %all-to-all-start.1 = ((bf16[4,128,1024]{2,1,0:T(8,128)(2,1)}), bf16[4,128,1024]{2,1,0:T(8,128)(2,1)}, u32[]{:S(2)}, u32[]{:S(2)}) async-start(bf16[4,128,1024]{2,1,0:T(8,128)(2,1)} %broadcast_in_dim.15), calls=%async_computation.1 | async-start | bytes 2097152 | tf_op jit(solution)/shard_map/all_to_all | solution.py:19
  297.2 6.7 %convolution_convert_fusion = bf16[4096,128]{1,0:T(8,128)(2,1)} fusion(bf16[4096,1024]{1,0:T(8,128)(2,1)} %bitcast.98, bf16[2,1024,1408]{2,1,0:T(8,128)(2,1)} %all-gather.3.cloned.1.call-done), kind=kOutput, calls=%fused_computation.9 | convolution fusion | flops 1074266112 | bytes 9699328 | tf_op jit(solution)/shard_map/dot_general | solution.py:34
  304.0 3.9 %reshape.1014 = bf16[2,2048,2,64]{3,2,1,0:T(2,128)(2,1)S(1)} reshape(bf16[4096,128]{1,0:T(8,128)(2,1)} %convolution_convert_fusion) | data formatting | bytes 2097152 | tf_op jit(solution)/shard_map/reshape | solution.py:99
  307.8 3.6 copy.52
  311.4 6.7 %convolution_convert_fusion.1 = bf16[4096,128]{1,0:T(8,128)(2,1)} fusion(bf16[4096,1024]{1,0:T(8,128)(2,1)} %bitcast.99, bf16[2,1024,1408]{2,1,0:T(8,128)(2,1)} %all-gather.3.cloned.1.call-done), kind=kOutput, calls=%fused_computation.10 | convolution fusion | flops 1074266112 | bytes 9699328 | tf_op jit(solution)/shard_map/dot_general | solution.py:34
  318.1 3.9 %reshape.1013 = bf16[2,2048,2,64]{3,2,1,0:T(2,128)(2,1)S(1)} reshape(bf16[4096,128]{1,0:T(8,128)(2,1)} %convolution_convert_fusion.1) | data formatting | bytes 2097152 | tf_op jit(solution)/shard_map/reshape | solution.py:106
  322.0 3.6 copy.49
  325.5 1.5 convert_reduce_fusion.2
  331.7 3.2 fusion.220
  335.0 2.5 fusion.16
  338.0 17.5 %all_to_all.20 = bf16[4,128,1024]{2,1,0:T(8,128)(2,1)S(1)} all-to-all(bf16[4,128,1024]{2,1,0:T(8,128)(2,1)S(1)} %broadcast_in_dim.16), channel_id=1, replica_groups=mesh['dp'=64,'mp'=4] {'mp'}, dimensions={0} | all-to-all | bytes 2097152 | tf_op jit(solution)/shard_map/all_to_all | solution.py:19
  356.4 4.4 %fusion.14 = bf16[128,1024]{1,0:T(8,128)(2,1)S(1)} fusion(bf16[2,1024,1024]{1,2,0:T(8,128)(2,1)} %all-gather.5.cloned.1.call-done, bf16[128,1024]{1,0:T(8,128)(2,1)S(1)} %bitcast.112, bf16[2,1024,1408]{2,1,0:T(8,128)(2,1)} %all-gather.3.cloned.1.call-done), kind=kOutput, calls=%fused_computation.32 | convolution fusion | flops 545521664 | bytes 4718592 | tf_op jit(solution)/shard_map/dot_general | solution.py:34
  361.0 16.9 %all_to_all.21 = bf16[4,128,1024]{2,1,0:T(8,128)(2,1)S(1)} all-to-all(bf16[4,128,1024]{2,1,0:T(8,128)(2,1)S(1)} %broadcast_in_dim.17), channel_id=1, replica_groups=mesh['dp'=64,'mp'=4] {'mp'}, dimensions={0} | all-to-all | bytes 2097152 | tf_op jit(solution)/shard_map/all_to_all | solution.py:19
  (81 shorter events, 18.8 us)
Async XLA Ops:
  6.5 206.8 %all-gather.3.cloned.1.call-start = ((), (), s32[]{:S(2)}) async-start(), calls=%async_computation.4 | async-start | bytes 5857280 | tf_op jit(solution)/shard_map/all_gather | solution.py:13
  8.1 279.4 %all-gather.5.cloned.1.call-start = ((), (), s32[]{:S(2)}) async-start(), calls=%async_computation.5 | async-start | bytes 4259840 | tf_op jit(solution)/shard_map/all_gather | solution.py:70
  13.3 5.8 %copy-start = (bf16[2,8,256,1024]{3,2,1,0:T(8,128)(2,1)S(1)}, bf16[2,8,256,1024]{3,2,1,0:T(8,128)(2,1)}, u32[]{:S(2)}) copy-start(bf16[2,8,256,1024]{3,2,1,0:T(8,128)(2,1)} %param.13) | copy-start | bytes 25165828
  19.0 3.4 copy-start.1
  251.5 5.4 %copy-start.2 = (f32[2,1024]{1,0:T(2,128)S(1)}, f32[2,1024]{1,0:T(2,128)}, u32[]{:S(2)}) copy-start(f32[2,1024]{1,0:T(2,128)} %param.18) | copy-start | bytes 24580
  253.1 17.9 %all-to-all-start = ((bf16[4,128,1024]{2,1,0:T(8,128)(2,1)}), bf16[4,128,1024]{2,1,0:T(8,128)(2,1)S(1)}, u32[]{:S(2)}, u32[]{:S(2)}) async-start(bf16[4,128,1024]{2,1,0:T(8,128)(2,1)} %broadcast_in_dim.13), calls=%async_computation | async-start | bytes 2097152 | tf_op jit(solution)/shard_map/all_to_all | solution.py:19
  293.0 32.6 %all-to-all-start.1 = ((bf16[4,128,1024]{2,1,0:T(8,128)(2,1)}), bf16[4,128,1024]{2,1,0:T(8,128)(2,1)}, u32[]{:S(2)}, u32[]{:S(2)}) async-start(bf16[4,128,1024]{2,1,0:T(8,128)(2,1)} %broadcast_in_dim.15), calls=%async_computation.1 | async-start | bytes 2097152 | tf_op jit(solution)/shard_map/all_to_all | solution.py:19
  360.8 17.7 %copy-start.3 = (f32[1024]{0:T(1024)S(1)}, f32[1024]{0:T(1024)}, u32[]{:S(2)}) copy-start(f32[1024]{0:T(1024)} %param.19) | copy-start | bytes 12292
Sparse Core Ops, SparseCore 0:
  11.0 137.5 all-gather.2
  152.1 135.3 all-gather.4
where the time goes:
time: 387 us; the launch traced here: 386 us
  blocking collectives  218 us (56%)
  matrix products  54.6 us (14%)
  local copies, waits for them, and re-layouts  36.3 us (9%)
  waiting for transfers between devices  30.4 us (8%)
  other arithmetic  25 us (6%)
  between operations  13.8 us (4%)
  starting transfers between devices  8.04 us (2%)
    all_gather x1, blocking collectives, on_device(): lax.all_gather(w_out, 'dp', axis=2, tiled=True)  184 us
    dot_general x14, matrix products, matmul(): return jnp.dot(left, right, preferred_element_type=jnp.float32)  43.1 us
    all_to_all x2, blocking collectives, copy_for_each(): return lax.all_to_all(copies, axis, split_axis=0, concat_axis=0, tiled=True)  34.3 us
    all_gather x1, waiting for transfers between devices, on_device(): lax.all_gather(w_down, 'dp', axis=2, tiled=True)  15.6 us
    reshape x4, local copies, waits for them, and re-layouts, on_device(): key_media.astype(jnp.bfloat16)  14.9 us
    reshape x4, local copies, waits for them, and re-layouts, on_device(): value_media.astype(jnp.bfloat16)  14.8 us
    all_to_all x2, waiting for transfers between devices, copy_for_each(): return lax.all_to_all(copies, axis, split_axis=0, concat_axis=0, tiled=True)  14.2 us
    all_to_all x2, starting transfers between devices, copy_for_each(): return lax.all_to_all(copies, axis, split_axis=0, concat_axis=0, tiled=True)  8 us
  transfers between devices with their start and end apart: 4, of which 2 were waited for; matrix products, arithmetic and copies ran while one was open for 23% of the time, Pallas kernels for 0%

commit v1 on v0

--- a/solution.py
+++ b/solution.py
@@ -66,7 +66,9 @@
     )
     row_parts = in_one_piece((w_query, w_key, w_value, w_up), "dp", 1, 2)
     col_parts = (
-        lax.all_gather(w_out, "dp", axis=2, tiled=True),
+        jnp.concatenate(
+            lax.all_to_all(jnp.stack([w_out] * lax.axis_size("dp")), "dp", 0, 0), axis=2
+        ),
         lax.all_gather(w_down, "dp", axis=2, tiled=True),
     )
 

time: 387 us -> 375 us (0.969)
  blocking collectives: 218 us -> 34.3 us
  waiting for transfers between devices: 30.4 us -> 185 us
  starting transfers between devices: 8.04 us -> 22.2 us
    all_gather x1 -> x0, blocking collectives: 184 us -> none  [on_device(): lax.all_gather(w_out, 'dp', axis=2, tiled=True)]
    all_gather x1, waiting for transfers between devices: 0.01 us -> 101 us  [in_one_piece(): filled = lax.all_gather(both, axis, axis=dim, tiled=True)]
    all_gather x1, waiting for transfers between devices: 15.6 us -> 67.2 us  [on_device(): lax.all_gather(w_down, 'dp', axis=2, tiled=True)]
    all_to_all x0 -> x1, starting transfers between devices: none -> 14.2 us  [on_device(): lax.all_to_all(jnp.stack([w_out] * lax.axis_size('dp')), 'dp', 0, 0)]
  transfers between devices with their start and end apart: 4 -> 5, of which waited for: 2 -> 3; matrix products, arithmetic and copies ran while one was open for 23% -> 24% of each run, Pallas kernels for 0% -> 0%
where the time goes in v1:
time: 375 us; the launch traced here: 372 us
  waiting for transfers between devices  185 us (49%)
  matrix products  52.2 us (14%)
  local copies, waits for them, and re-layouts  39.5 us (11%)
  blocking collectives  34.3 us (9%)
  other arithmetic  25.1 us (7%)
  starting transfers between devices  22.2 us (6%)
  between operations  13.8 us (4%)
    all_gather x1, waiting for transfers between devices, in_one_piece(): filled = lax.all_gather(both, axis, axis=dim, tiled=True)  101 us
    all_gather x1, waiting for transfers between devices, on_device(): lax.all_gather(w_down, 'dp', axis=2, tiled=True)  67.2 us
    dot_general x14, matrix products, matmul(): return jnp.dot(left, right, preferred_element_type=jnp.float32)  43.1 us
    all_to_all x2, blocking collectives, copy_for_each(): return lax.all_to_all(copies, axis, split_axis=0, concat_axis=0, tiled=True)  34.3 us
    all_to_all x2, waiting for transfers between devices, copy_for_each(): return lax.all_to_all(copies, axis, split_axis=0, concat_axis=0, tiled=True)  16.1 us
    reshape x4, local copies, waits for them, and re-layouts, on_device(): value_media.astype(jnp.bfloat16)  14.9 us
    reshape x4, local copies, waits for them, and re-layouts, on_device(): key_media.astype(jnp.bfloat16)  14.9 us
    all_to_all x1, starting transfers between devices, on_device(): lax.all_to_all(jnp.stack([w_out] * lax.axis_size('dp')), 'dp', 0, 0)  14.2 us
  transfers between devices with their start and end apart: 5, of which 3 were waited for; matrix products, arithmetic and copies ran while one was open for 24% of the time, Pallas kernels for 0%

profile of v1, /device:TPU:32, one launch (start us, length us, event | category | flops | bytes accessed | tf_op | source)
XLA Modules:
  0.0 372.3 jit_solution(3923963577337899368)
XLA Ops:
  6.5 1.5 pad_maximum_fusion
  8.1 1.6 stack.2
  9.6 14.2 %all-to-all-start = ((bf16[64,2,128,16]{2,3,1,0:T(8,128)(2,1)}), bf16[64,2,128,16]{2,3,1,0:T(8,128)(2,1)S(1)}, u32[]{:S(2)}, u32[]{:S(2)}) async-start(bf16[64,2,128,16]{2,3,1,0:T(8,128)(2,1)} %stack.2), calls=%async_computation | async-start | bytes 1048576 | tf_op jit(solution)/shard_map/all_to_all | solution.py:70
  29.1 5.3 %fusion.3 = f32[2,8,256]{2,1,0:T(8,128)S(1)} fusion(bf16[2,8,256,1024]{3,2,1,0:T(8,128)(2,1)} %param.13, f32[8,1024]{1,0:T(8,128)S(1)} %convert_element_type.171), kind=kLoop, calls=%fused_computation.7 | loop fusion | flops 12578816 | bytes 8437760 | tf_op jit(solution)/shard_map/reduce_sum | solution.py:28
  34.9 3.2 multiply_reduce_fusion
  38.2 7.3 %multiply_convert_fusion = (bf16[2,8,256,1024]{3,2,1,0:T(8,128)(2,1)}, bf16[2,8,256,1024]{3,2,1,0:T(8,128)(2,1)}) fusion(bf16[2,8,256,1024]{3,2,1,0:T(8,128)(2,1)S(1)} %copy-done, f32[1024]{0:T(1024)S(1)} %bitcast.122, f32[2,8,256]{2,1,0:T(8,128)S(1)} %add_rsqrt_fusion, f32[2,8,256]{2,1,0:T(8,128)S(1)} %broadcast_multiply_fusion, ...), kind=kLoop, calls=%fused_computation.2 | loop fusion | flops 33554432 | bytes 25239552 | tf_op jit(solution)/shard_map/convert_element_type | solution.py:89
  46.4 101.1 %all-gather.3.cloned.1.call-done = bf16[2,1024,1408]{2,1,0:T(8,128)(2,1)} async-done(((bf16[2,16,1408]{2,1,0:T(8,128)(2,1)}), bf16[2,1024,1408]{2,1,0:T(8,128)(2,1)}) %all-gather.3.cloned.1.call-update) | async-done | bytes 5767184 | tf_op jit(solution)/shard_map/all_gather | solution.py:13
  150.1 6.7 %convolution_convert_fusion.2 = bf16[4096,128]{1,0:T(8,128)(2,1)} fusion(bf16[4096,1024]{1,0:T(8,128)(2,1)} %bitcast.101, bf16[2,1024,1408]{2,1,0:T(8,128)(2,1)} %all-gather.3.cloned.1.call-done), kind=kOutput, calls=%fused_computation.11 | convolution fusion | flops 1074266112 | bytes 9699328 | tf_op jit(solution)/shard_map/dot_general | solution.py:34
  156.8 3.9 %reshape.1023 = bf16[2,2048,2,64]{3,2,1,0:T(2,128)(2,1)S(1)} reshape(bf16[4096,128]{1,0:T(8,128)(2,1)} %convolution_convert_fusion.2) | data formatting | bytes 2097152 | tf_op jit(solution)/shard_map/reshape | solution.py:101
  160.7 3.6 copy.62
  166.3 6.7 %convolution_convert_fusion.3 = bf16[4096,128]{1,0:T(8,128)(2,1)} fusion(bf16[4096,1024]{1,0:T(8,128)(2,1)} %bitcast.102, bf16[2,1024,1408]{2,1,0:T(8,128)(2,1)} %all-gather.3.cloned.1.call-done), kind=kOutput, calls=%fused_computation.12 | convolution fusion | flops 1074266112 | bytes 9699328 | tf_op jit(solution)/shard_map/dot_general | solution.py:34
  173.0 4.0 %reshape.1022 = bf16[2,2048,2,64]{3,2,1,0:T(2,128)(2,1)S(1)} reshape(bf16[4096,128]{1,0:T(8,128)(2,1)} %convolution_convert_fusion.3) | data formatting | bytes 2097152 | tf_op jit(solution)/shard_map/reshape | solution.py:108
  177.0 3.5 copy.59
  180.5 2.0 fusion.216
  182.5 2.5 fusion.15
  186.7 3.7 %all-to-all-start.1 = ((bf16[4,128,1024]{2,1,0:T(8,128)(2,1)}), bf16[4,128,1024]{2,1,0:T(8,128)(2,1)S(1)}, u32[]{:S(2)}, u32[]{:S(2)}) async-start(bf16[4,128,1024]{2,1,0:T(8,128)(2,1)} %broadcast_in_dim.13), calls=%async_computation.1 | async-start | bytes 2097152 | tf_op jit(solution)/shard_map/all_to_all | solution.py:19
  190.5 16.1 %all-to-all-done.1 = bf16[4,128,1024]{2,1,0:T(8,128)(2,1)S(1)} async-done(((bf16[4,128,1024]{2,1,0:T(8,128)(2,1)}), bf16[4,128,1024]{2,1,0:T(8,128)(2,1)S(1)}, u32[]{:S(2)}, u32[]{:S(2)}) %all-to-all-start.1) | async-done | bytes 1048608 | tf_op jit(solution)/shard_map/all_to_all | solution.py:19
  207.4 67.2 %all-gather.5.cloned.1.call-done = bf16[2,1024,1024]{1,2,0:T(8,128)(2,1)} async-done(((bf16[2,1024,16]{1,2,0:T(8,128)(2,1)}), bf16[2,1024,1024]{1,2,0:T(8,128)(2,1)}) %all-gather.5.cloned.1.call-update) | async-done | bytes 4194320 | tf_op jit(solution)/shard_map/all_gather | solution.py:72
  274.6 4.4 %fusion.13 = bf16[128,1024]{1,0:T(8,128)(2,1)S(1)} fusion(bf16[2,1024,1024]{1,2,0:T(8,128)(2,1)} %all-gather.5.cloned.1.call-done, bf16[128,1024]{1,0:T(8,128)(2,1)S(1)} %bitcast.117, bf16[2,1024,1408]{2,1,0:T(8,128)(2,1)} %all-gather.3.cloned.1.call-done), kind=kOutput, calls=%fused_computation.31 | convolution fusion | flops 545521664 | bytes 4718592 | tf_op jit(solution)/shard_map/dot_general | solution.py:34
  280.1 4.2 %all-to-all-start.2 = ((bf16[4,128,1024]{2,1,0:T(8,128)(2,1)}), bf16[4,128,1024]{2,1,0:T(8,128)(2,1)}, u32[]{:S(2)}, u32[]{:S(2)}) async-start(bf16[4,128,1024]{2,1,0:T(8,128)(2,1)} %broadcast_in_dim.15), calls=%async_computation.2 | async-start | bytes 2097152 | tf_op jit(solution)/shard_map/all_to_all | solution.py:19
  284.4 6.7 %convolution_convert_fusion = bf16[4096,128]{1,0:T(8,128)(2,1)} fusion(bf16[4096,1024]{1,0:T(8,128)(2,1)} %bitcast.99, bf16[2,1024,1408]{2,1,0:T(8,128)(2,1)} %all-gather.3.cloned.1.call-done), kind=kOutput, calls=%fused_computation.9 | convolution fusion | flops 1074266112 | bytes 9699328 | tf_op jit(solution)/shard_map/dot_general | solution.py:34
  291.1 3.9 %reshape.1025 = bf16[2,2048,2,64]{3,2,1,0:T(2,128)(2,1)S(1)} reshape(bf16[4096,128]{1,0:T(8,128)(2,1)} %convolution_convert_fusion) | data formatting | bytes 2097152 | tf_op jit(solution)/shard_map/reshape | solution.py:101
  295.0 3.6 copy.71
  298.5 6.7 %convolution_convert_fusion.1 = bf16[4096,128]{1,0:T(8,128)(2,1)} fusion(bf16[4096,1024]{1,0:T(8,128)(2,1)} %bitcast.100, bf16[2,1024,1408]{2,1,0:T(8,128)(2,1)} %all-gather.3.cloned.1.call-done), kind=kOutput, calls=%fused_computation.10 | convolution fusion | flops 1074266112 | bytes 9699328 | tf_op jit(solution)/shard_map/dot_general | solution.py:34
  305.2 3.9 %reshape.1024 = bf16[2,2048,2,64]{3,2,1,0:T(2,128)(2,1)S(1)} reshape(bf16[4096,128]{1,0:T(8,128)(2,1)} %convolution_convert_fusion.1) | data formatting | bytes 2097152 | tf_op jit(solution)/shard_map/reshape | solution.py:108
  309.1 3.6 copy.68
  312.7 1.5 convert_reduce_fusion.2
  319.0 2.0 fusion.221
  321.0 2.5 fusion.16
  324.1 17.5 %all_to_all.25 = bf16[4,128,1024]{2,1,0:T(8,128)(2,1)S(1)} all-to-all(bf16[4,128,1024]{2,1,0:T(8,128)(2,1)S(1)} %broadcast_in_dim.16), channel_id=1, replica_groups=mesh['dp'=64,'mp'=4] {'mp'}, dimensions={0} | all-to-all | bytes 2097152 | tf_op jit(solution)/shard_map/all_to_all | solution.py:19
  342.5 4.4 %fusion.14 = bf16[128,1024]{1,0:T(8,128)(2,1)S(1)} fusion(bf16[2,1024,1024]{1,2,0:T(8,128)(2,1)} %all-gather.5.cloned.1.call-done, bf16[128,1024]{1,0:T(8,128)(2,1)S(1)} %bitcast.116, bf16[2,1024,1408]{2,1,0:T(8,128)(2,1)} %all-gather.3.cloned.1.call-done), kind=kOutput, calls=%fused_computation.32 | convolution fusion | flops 545521664 | bytes 4718592 | tf_op jit(solution)/shard_map/dot_general | solution.py:34
  347.0 16.9 %all_to_all.26 = bf16[4,128,1024]{2,1,0:T(8,128)(2,1)S(1)} all-to-all(bf16[4,128,1024]{2,1,0:T(8,128)(2,1)S(1)} %broadcast_in_dim.17), channel_id=1, replica_groups=mesh['dp'=64,'mp'=4] {'mp'}, dimensions={0} | all-to-all | bytes 2097152 | tf_op jit(solution)/shard_map/all_to_all | solution.py:19
  (91 shorter events, 22.7 us)
Async XLA Ops:
  6.5 140.9 %all-gather.3.cloned.1.call-start = ((), (), s32[]{:S(2)}) async-start(), calls=%async_computation.5 | async-start | bytes 5857280 | tf_op jit(solution)/shard_map/all_gather | solution.py:13
  9.6 35.9 %all-to-all-start = ((bf16[64,2,128,16]{2,3,1,0:T(8,128)(2,1)}), bf16[64,2,128,16]{2,3,1,0:T(8,128)(2,1)S(1)}, u32[]{:S(2)}, u32[]{:S(2)}) async-start(bf16[64,2,128,16]{2,3,1,0:T(8,128)(2,1)} %stack.2), calls=%async_computation | async-start | bytes 1048576 | tf_op jit(solution)/shard_map/all_to_all | solution.py:70
  23.8 250.8 %all-gather.5.cloned.1.call-start = ((), (), s32[]{:S(2)}) async-start(), calls=%async_computation.6 | async-start | bytes 4259840 | tf_op jit(solution)/shard_map/all_gather | solution.py:72
  29.1 5.8 %copy-start = (bf16[2,8,256,1024]{3,2,1,0:T(8,128)(2,1)S(1)}, bf16[2,8,256,1024]{3,2,1,0:T(8,128)(2,1)}, u32[]{:S(2)}) copy-start(bf16[2,8,256,1024]{3,2,1,0:T(8,128)(2,1)} %param.13) | copy-start | bytes 25165828
  173.0 7.5 %copy-start.2 = (bf16[2,2048,2,64]{1,3,2,0:T(8,128)(2,1)S(1)}, bf16[2,2048,2,64]{1,3,2,0:T(8,128)(2,1)}, u32[]{:S(2)}) copy-start(bf16[2,2048,2,64]{1,3,2,0:T(8,128)(2,1)} %copy.62) | copy-start | bytes 3145732
  182.5 2.8 copy-start.4
  185.1 5.4 %copy-start.5 = (f32[2,1024]{1,0:T(2,128)S(1)}, f32[2,1024]{1,0:T(2,128)}, u32[]{:S(2)}) copy-start(f32[2,1024]{1,0:T(2,128)} %param.18) | copy-start | bytes 24580
  186.7 19.9 %all-to-all-start.1 = ((bf16[4,128,1024]{2,1,0:T(8,128)(2,1)}), bf16[4,128,1024]{2,1,0:T(8,128)(2,1)S(1)}, u32[]{:S(2)}, u32[]{:S(2)}) async-start(bf16[4,128,1024]{2,1,0:T(8,128)(2,1)} %broadcast_in_dim.13), calls=%async_computation.1 | async-start | bytes 2097152 | tf_op jit(solution)/shard_map/all_to_all | solution.py:19
  280.1 32.6 %all-to-all-start.2 = ((bf16[4,128,1024]{2,1,0:T(8,128)(2,1)}), bf16[4,128,1024]{2,1,0:T(8,128)(2,1)}, u32[]{:S(2)}, u32[]{:S(2)}) async-start(bf16[4,128,1024]{2,1,0:T(8,128)(2,1)} %broadcast_in_dim.15), calls=%async_computation.2 | async-start | bytes 2097152 | tf_op jit(solution)/shard_map/all_to_all | solution.py:19
  312.7 6.3 %copy-start.1 = (bf16[2,2048,2,64]{1,3,2,0:T(8,128)(2,1)S(1)}, bf16[2,2048,2,64]{1,3,2,0:T(8,128)(2,1)}, u32[]{:S(2)}) copy-start(bf16[2,2048,2,64]{1,3,2,0:T(8,128)(2,1)} %copy.71) | copy-start | bytes 3145732
  321.0 2.7 copy-start.3
  346.8 17.7 %copy-start.6 = (f32[1024]{0:T(1024)S(1)}, f32[1024]{0:T(1024)}, u32[]{:S(2)}) copy-start(f32[1024]{0:T(1024)} %param.19) | copy-start | bytes 12292
Sparse Core Ops, SparseCore 0:
  11.0 136.4 all-gather.2
  151.0 123.5 all-gather.4
